TPU v7x, 256 devices: a whole 4x4x8 slice. The times are simulated.
256 devices in a mesh: seq: 32 (over x, z_hi, y), rep: 8 (over z_lo, core).
Axes of the slice: x: 4, y: 4, z: 8 (z_hi: 2, z_lo: 4; z = z_hi * 4 + z_lo), core: 2. Of those that a mesh axis runs over, the one named last changes fastest.
Arguments:
- tokens: bfloat16 [16, 96, 180, 768], P('rep', 'seq'), may hold values from -6 to 6
- cotangent: bfloat16 [16, 96, 180, 768], P('rep', 'seq'), may hold values from -6 to 6
- in_weight: bfloat16 [2, 8, 96, 96], replicated, may hold values from -0.21875 to 0.21875
- in_bias: float32 [2, 768], replicated, may hold values from -0.6 to 0.6
- out_weight: bfloat16 [2, 8, 96, 96], replicated, may hold values from -0.21875 to 0.21875
- out_bias: float32 [2, 768], replicated, may hold values from -0.12 to 0.12
Outputs:
- mixed_out: bfloat16 [16, 96, 180, 768], P('rep', 'seq')
- tokens_grad: bfloat16 [16, 96, 180, 768], P('rep', 'seq')
- in_weight_grad: float32 [2, 8, 96, 96], replicated
- in_bias_grad: float32 [2, 768], replicated
- out_weight_grad: float32 [2, 8, 96, 96], replicated
- out_bias_grad: float32 [2, 768], replicated
All inputs are finite; a program needn't handle non-finite values.
Results may differ from a plain program's by a relative error of at most 0.0094.
Values may be sent and summed in bfloat16 or wider, within the bound.
A program may use at most 64 MiB of HBM per device.

v0:
```python
import math

import jax
import jax.numpy as jnp
from jax import lax
from jax.sharding import PartitionSpec as P

BLOCKS = 8
BLOCK = 96
MODES = 64


def packed_total(arrays, axis):
    ravelled, at, done = (jnp.concatenate([a.reshape(-1) for a in arrays]), 0, [])
    running = lax.psum(ravelled, axis)
    for a in arrays:
        done.append(running[at : at + a.size].reshape(a.shape))
        at += a.size
    return tuple(done)


def grid_tables(length, modes):
    position = jnp.arange(length, dtype=jnp.int32)
    frequency = jnp.arange(modes, dtype=jnp.int32)
    residue = position[:, None] * frequency[None, :] % length
    angles = residue.astype(jnp.float32) * (2.0 * math.pi / length)
    factor = 1.0 / math.sqrt(length)
    cosine_table = (jnp.cos(angles) * factor).astype(jnp.bfloat16)
    sine_table = (jnp.sin(angles) * factor).astype(jnp.bfloat16)
    return (cosine_table, sine_table)


def column_tables(grid_width, modes):
    cosine_table, sine_table = grid_tables(grid_width, modes)
    forward = jnp.stack([cosine_table, -sine_table], axis=2)
    doubling = jnp.where(jnp.arange(modes) == 0, 1.0, 2.0).astype(jnp.bfloat16)[:, None]
    inverse = jnp.stack([cosine_table.T * doubling, -(sine_table.T * doubling)], axis=1)
    return (forward, inverse)


def row_table(length):
    cosine_table, sine_table = grid_tables(length, length)
    upper_rows = jnp.stack([cosine_table, sine_table], axis=2)
    lower_rows = jnp.stack([-sine_table, cosine_table], axis=2)
    return jnp.stack([upper_rows, lower_rows], axis=1)


def block_weights(weight):
    real_part, imag_part = (weight[0], weight[1])
    upper_half = jnp.stack([real_part, imag_part], axis=2)
    lower_half = jnp.stack([-imag_part, real_part], axis=2)
    return jnp.stack([upper_half, lower_half], axis=1)


def fold_blocks(blockwise):
    real_part = blockwise[:, 0, :, 0, :] + blockwise[:, 1, :, 1, :]
    imag_part = blockwise[:, 0, :, 1, :] - blockwise[:, 1, :, 0, :]
    return jnp.stack([real_part, imag_part])


def mix_forward(spectrum, weights_in, weights_out, bias_in, bias_out):
    mode_count = spectrum.shape[0] * spectrum.shape[1] * spectrum.shape[2]
    flat_modes = spectrum.reshape(mode_count, 2, BLOCKS, BLOCK)
    hidden_pre = (
        jnp.einsum("mcbi,bciej->mebj", flat_modes, weights_in, preferred_element_type=jnp.float32)
        + bias_in
    )
    hidden = jax.nn.gelu(hidden_pre).astype(jnp.bfloat16)
    spectrum_out = (
        jnp.einsum("mcbi,bciej->mebj", hidden, weights_out, preferred_element_type=jnp.float32)
        + bias_out
    )
    return (
        flat_modes,
        hidden_pre,
        hidden,
        spectrum_out.astype(jnp.bfloat16).reshape(spectrum.shape),
    )


def mix_backward(flat_modes, hidden_pre, hidden, incoming, weights_in, weights_out):
    incoming_flat = incoming.reshape(flat_modes.shape)
    out_bias_part = jnp.sum(incoming_flat.astype(jnp.float32), axis=0).reshape(2, -1)
    out_weight_part = fold_blocks(
        jnp.einsum("mcbi,mebj->bciej", hidden, incoming_flat, preferred_element_type=jnp.float32)
    )
    hidden_grad = jnp.einsum(
        "mebj,bciej->mcbi", incoming_flat, weights_out, preferred_element_type=jnp.float32
    )
    pre_grad = jax.vjp(jax.nn.gelu, hidden_pre)[1](hidden_grad)[0].astype(jnp.bfloat16)
    in_bias_part = jnp.sum(pre_grad.astype(jnp.float32), axis=0).reshape(2, -1)
    in_weight_part = fold_blocks(
        jnp.einsum("mcbi,mebj->bciej", flat_modes, pre_grad, preferred_element_type=jnp.float32)
    )
    spectrum_grad = jnp.einsum(
        "mebj,bciej->mcbi", pre_grad, weights_in, preferred_element_type=jnp.float32
    )
    spectrum_grad = spectrum_grad.astype(jnp.bfloat16).reshape(incoming.shape)
    return (spectrum_grad, (in_weight_part, in_bias_part, out_weight_part, out_bias_part))


def shards(tokens, cotangent, in_weight, in_bias, out_weight, out_bias):
    samples, row_count, grid_width, channels = tokens.shape
    length = row_count * lax.axis_size("seq")
    column_forward, column_inverse = column_tables(grid_width, MODES)
    row_matrix = row_table(length)
    weights_in = block_weights(in_weight)
    weights_out = block_weights(out_weight)
    bias_in = in_bias.reshape(2, BLOCKS, BLOCK)
    bias_out = out_bias.reshape(2, BLOCKS, BLOCK)

    def along_rows(section):
        return jnp.einsum(
            "qehc,shkcd->sqked", row_matrix, section, preferred_element_type=jnp.float32
        ).astype(jnp.bfloat16)

    def back_rows(section):
        return jnp.einsum(
            "qehc,sqked->shkcd", row_matrix, section, preferred_element_type=jnp.float32
        ).astype(jnp.bfloat16)

    spec_rows = jnp.einsum(
        "shwd,wkc->shkcd", tokens, column_forward, preferred_element_type=jnp.float32
    ).astype(jnp.bfloat16)
    cot_rows = jnp.einsum(
        "shwd,kcw->shkcd", cotangent, column_inverse, preferred_element_type=jnp.float32
    ).astype(jnp.bfloat16)
    sections = (
        lax.all_to_all(spec_rows, "seq", split_axis=2, concat_axis=1, tiled=True),
        lax.all_to_all(cot_rows, "seq", split_axis=2, concat_axis=1, tiled=True),
    )
    spectrum = along_rows(sections[0])
    incoming = along_rows(sections[1])
    flat_modes, hidden_pre, hidden, spectrum_out = mix_forward(
        spectrum, weights_in, weights_out, bias_in, bias_out
    )
    spectrum_grad, partials = mix_backward(
        flat_modes, hidden_pre, hidden, incoming, weights_in, weights_out
    )
    sections = (
        lax.all_to_all(back_rows(spectrum_out), "seq", split_axis=1, concat_axis=2, tiled=True),
        lax.all_to_all(back_rows(spectrum_grad), "seq", split_axis=1, concat_axis=2, tiled=True),
    )
    mixed_grid = jnp.einsum(
        "shkcd,kcw->shwd", sections[0], column_inverse, preferred_element_type=jnp.float32
    )
    adjoint_part = jnp.einsum(
        "shkcd,wkc->shwd", sections[1], column_forward, preferred_element_type=jnp.float32
    )
    mixed_out = (tokens.astype(jnp.float32) + mixed_grid).astype(jnp.bfloat16)
    tokens_grad = (cotangent.astype(jnp.float32) + adjoint_part).astype(jnp.bfloat16)
    totals = packed_total((partials[0], partials[1], partials[2], partials[3]), ("seq", "rep"))
    divisor = float(samples * lax.axis_size("rep"))
    return (
        mixed_out,
        tokens_grad,
        totals[0] / divisor,
        totals[1] / divisor,
        totals[2] / divisor,
        totals[3] / divisor,
    )


def solution(mesh):
    in_specs = (P("rep", "seq", None, None), P("rep", "seq", None, None), P(), P(), P(), P())
    out_specs = (P("rep", "seq", None, None), P("rep", "seq", None, None), P(), P(), P(), P())
    return jax.shard_map(shards, mesh=mesh, in_specs=in_specs, out_specs=out_specs, check_vma=False)
```

profile of v0, /device:TPU:1, one launch (start us, length us, event | category | flops | bytes accessed | tf_op | source)
XLA Modules:
  0.0 449.5 jit_solution(11837044986318811130)
XLA Ops:
  7.7 1.9 fusion.32
  9.7 2.2 copy.175
  11.9 14.6 %all-to-all-start = ((bf16[2,3,64,2,768]{4,3,1,0,2:T(2,128)(2,1)}), bf16[2,3,64,2,768]{4,3,1,0,2:T(2,128)(2,1)S(1)}, u32[]{:S(2)}, u32[]{:S(2)}) async-start(bf16[2,3,64,2,768]{4,3,1,0,2:T(2,128)(2,1)} %copy.175), calls=%async_computation | async-start | bytes 2359296 | tf_op jit(solution)/shard_map/all_to_all | solution.py:129
  28.0 2.2 copy.190
  30.2 19.5 %all-to-all-done = bf16[2,3,64,2,768]{4,3,1,0,2:T(2,128)(2,1)S(1)} async-done(((bf16[2,3,64,2,768]{4,3,1,0,2:T(2,128)(2,1)}), bf16[2,3,64,2,768]{4,3,1,0,2:T(2,128)(2,1)S(1)}, u32[]{:S(2)}, u32[]{:S(2)}) %all-to-all-start) | async-done | bytes 1179680 | tf_op jit(solution)/shard_map/all_to_all | solution.py:129
  49.7 4.9 %all-to-all-start.2 = ((bf16[2,3,64,2,768]{4,3,1,0,2:T(2,128)(2,1)}), bf16[2,3,64,2,768]{4,3,1,0,2:T(2,128)(2,1)}, u32[]{:S(2)}, u32[]{:S(2)}) async-start(bf16[2,3,64,2,768]{4,3,1,0,2:T(2,128)(2,1)} %copy.190), calls=%async_computation.2 | async-start | bytes 2359296 | tf_op jit(solution)/shard_map/all_to_all | solution.py:130
  60.9 2.1 maximum_bitcast_fusion.2
  65.5 2.2 copy.178
  67.7 3.7 reshape.411
  71.4 2.1 copy.191
  74.0 2.2 copy.193
  76.3 4.6 %reshape.413 = bf16[384,2,8,96]{3,2,1,0:T(8,128)(2,1)} reshape(bf16[2,96,2,2,768]{4,3,2,1,0:T(2,128)(2,1)} %copy.193) | data formatting | bytes 2359296 | tf_op jit(solution)/shard_map/reshape | solution.py:82
  80.8 2.8 copy.229
  83.6 2.0 fusion.19
  85.7 2.7 convert_reduce_fusion.1
  96.2 2.3 copy.197
  98.5 3.1 reshape.414
  101.6 1.8 fusion.39
  103.4 2.2 copy.200
  105.6 12.0 %all-to-all-start.3 = ((bf16[2,96,2,2,768]{4,3,2,0,1:T(2,128)(2,1)}), bf16[2,96,2,2,768]{4,3,2,0,1:T(2,128)(2,1)}, u32[]{:S(2)}, u32[]{:S(2)}) async-start(bf16[2,96,2,2,768]{4,3,2,0,1:T(2,128)(2,1)} %copy.200), calls=%async_computation.3 | async-start | bytes 2359296 | tf_op jit(solution)/shard_map/all_to_all | solution.py:142
  118.8 4.3 fusion.12
  123.2 2.5 copy.182
  125.7 3.1 reshape.412
  130.6 2.2 copy.185
  133.2 11.3 %all-to-all-start.1 = ((bf16[2,96,2,2,768]{4,3,2,0,1:T(2,128)(2,1)}), bf16[2,96,2,2,768]{4,3,2,0,1:T(2,128)(2,1)}, u32[]{:S(2)}, u32[]{:S(2)}) async-start(bf16[2,96,2,2,768]{4,3,2,0,1:T(2,128)(2,1)} %copy.185), calls=%async_computation.1 | async-start | bytes 2359296 | tf_op jit(solution)/shard_map/all_to_all | solution.py:141
  144.5 273.3 %all-reduce.2.cloned.1.call-done = f32[297984]{0:T(1024)} async-done(((f32[297984]{0:T(1024)}), f32[297984]{0:T(1024)}) %all-reduce.2.cloned.1.call-update) | async-done | bytes 1191952 | tf_op jit(solution)/shard_map/psum | solution.py:15
  423.3 3.3 copy.202
  426.6 3.0 all_to_all.67
  430.2 2.5 copy.211
  432.7 3.3 copy.187
  436.0 3.1 all_to_all.59
  439.8 2.5 copy.210
  (97 shorter events, 29.1 us)
Async XLA Ops:
  7.4 2.2 copy-start.16
  7.7 2.0 copy-start.18
  11.9 15.6 %copy-start = (bf16[2,3,180,768]{3,0,2,1:T(2,128)(2,1)S(1)}, bf16[2,3,180,768]{3,0,2,1:T(2,128)(2,1)}, u32[]{:S(2)}) copy-start(bf16[2,3,180,768]{3,0,2,1:T(2,128)(2,1)} %param.7) | copy-start | bytes 4976644
  11.9 37.8 %all-to-all-start = ((bf16[2,3,64,2,768]{4,3,1,0,2:T(2,128)(2,1)}), bf16[2,3,64,2,768]{4,3,1,0,2:T(2,128)(2,1)S(1)}, u32[]{:S(2)}, u32[]{:S(2)}) async-start(bf16[2,3,64,2,768]{4,3,1,0,2:T(2,128)(2,1)} %copy.175), calls=%async_computation | async-start | bytes 2359296 | tf_op jit(solution)/shard_map/all_to_all | solution.py:129
  26.9 0.6 copy-start.12
  26.9 0.6 copy-start.14
  49.7 21.6 %all-to-all-start.2 = ((bf16[2,3,64,2,768]{4,3,1,0,2:T(2,128)(2,1)}), bf16[2,3,64,2,768]{4,3,1,0,2:T(2,128)(2,1)}, u32[]{:S(2)}, u32[]{:S(2)}) async-start(bf16[2,3,64,2,768]{4,3,1,0,2:T(2,128)(2,1)} %copy.190), calls=%async_computation.2 | async-start | bytes 2359296 | tf_op jit(solution)/shard_map/all_to_all | solution.py:130
  54.6 5.6 %copy-start.20 = (f32[2,768]{1,0:T(2,128)S(1)}, f32[2,768]{1,0:T(2,128)}, u32[]{:S(2)}) copy-start(f32[2,768]{1,0:T(2,128)} %param.9) | copy-start | bytes 18436
  54.6 5.7 %copy-start.21 = (f32[2,768]{1,0:T(2,128)S(1)}, f32[2,768]{1,0:T(2,128)}, u32[]{:S(2)}) copy-start(f32[2,768]{1,0:T(2,128)} %param.11) | copy-start | bytes 18436
  60.2 2.8 copy-start.8
  83.6 2.0 copy-start.7
  83.6 2.0 copy-start.9
  83.6 2.0 copy-start.11
  85.6 3.7 copy-start.4
  90.6 1.0 copy-start.2
  90.6 1.1 copy-start.3
  105.6 12.1 %copy-start.5 = (f32[147456]{0:T(1024)S(1)}, f32[147456]{0:T(1024)}, u32[]{:S(2)}) copy-start(f32[147456]{0:T(1024)} %reshape.415) | copy-start | bytes 1769476
  105.6 12.1 %copy-start.6 = (f32[147456]{0:T(1024)S(1)}, f32[147456]{0:T(1024)}, u32[]{:S(2)}) copy-start(f32[147456]{0:T(1024)} %reshape.416) | copy-start | bytes 1769476
  105.6 27.6 %all-to-all-start.3 = ((bf16[2,96,2,2,768]{4,3,2,0,1:T(2,128)(2,1)}), bf16[2,96,2,2,768]{4,3,2,0,1:T(2,128)(2,1)}, u32[]{:S(2)}, u32[]{:S(2)}) async-start(bf16[2,96,2,2,768]{4,3,2,0,1:T(2,128)(2,1)} %copy.200), calls=%async_computation.3 | async-start | bytes 2359296 | tf_op jit(solution)/shard_map/all_to_all | solution.py:142
  117.6 1.2 copy-start.10
  117.6 300.1 %all-reduce.2.cloned.1.call-start = ((), (), s32[]{:S(2)}) async-start(), calls=%async_computation.4 | async-start | bytes 2383872 | tf_op jit(solution)/shard_map/psum | solution.py:15
  133.2 299.5 %all-to-all-start.1 = ((bf16[2,96,2,2,768]{4,3,2,0,1:T(2,128)(2,1)}), bf16[2,96,2,2,768]{4,3,2,0,1:T(2,128)(2,1)}, u32[]{:S(2)}, u32[]{:S(2)}) async-start(bf16[2,96,2,2,768]{4,3,2,0,1:T(2,128)(2,1)} %copy.185), calls=%async_computation.1 | async-start | bytes 2359296 | tf_op jit(solution)/shard_map/all_to_all | solution.py:141
  426.6 3.0 copy-start.17
  426.6 3.0 copy-start.19
  436.0 3.1 copy-start.1
  436.0 3.1 copy-start.13
  436.0 3.1 copy-start.15
Sparse Core Ops, SparseCore 0:
  124.4 293.3 all-reduce.1
where the time goes:
time: 455 us; the launch traced here: 450 us
  waiting for transfers between devices  293 us (64%)
  local copies, waits for them, and re-layouts  69.5 us (15%)
  starting transfers between devices  42.8 us (9%)
  matrix products  21.1 us (5%)
  between operations  15 us (3%)
  other arithmetic  7.98 us (2%)
    psum x1, waiting for transfers between devices, packed_total(): running = lax.psum(ravelled, axis)  273 us
    all_to_all x1, waiting for transfers between devices, shards(): lax.all_to_all(spec_rows, 'seq', split_axis=2, concat_axis=1, tiled=True)  19.5 us
    all_to_all x1, starting transfers between devices, shards(): lax.all_to_all(spec_rows, 'seq', split_axis=2, concat_axis=1, tiled=True)  14.6 us
    all_to_all x1, starting transfers between devices, shards(): lax.all_to_all(back_rows(spectrum_grad), 'seq', split_axis=1, concat_axis...  12 us
    all_to_all x1, starting transfers between devices, shards(): lax.all_to_all(back_rows(spectrum_out), 'seq', split_axis=1, concat_axis=...  11.3 us
    unnamed x50, local copies, waits for them, and re-layouts  9.42 us
  transfers between devices with their start and end apart: 5, of which 3 were waited for; matrix products, arithmetic and copies ran while one was open for 10% of the time, Pallas kernels for 0%

commit v1 on v0

v1 whole, which is shorter than its diff:
```python
import functools
import math

import jax
import jax.numpy as jnp
import numpy as np
from jax import lax
from jax.experimental import pallas as pl
from jax.experimental.pallas import tpu as pltpu
from jax.sharding import PartitionSpec as P

BF = jnp.bfloat16
F32 = jnp.float32
MESH = pl.DeviceIdType.MESH

SLOTS = 32
PLANE = 16
PIECE = 24
ALL = SLOTS * PIECE
D = 768
HALF = 384
COLS = 180
PADC = 192
ROWS = 96
NT = (((1,), (1,)), ((), ()))
TN = (((0,), (0,)), ((), ()))


def tables(length, modes):
    residue = np.arange(length)[:, None] * np.arange(modes)[None, :] % length
    angles = residue.astype(np.float32) * np.float32(2.0 * math.pi / length)
    factor = np.float32(1.0 / math.sqrt(length))
    return np.cos(angles) * factor, np.sin(angles) * factor


def constants():
    cos_c, sin_c = tables(COLS, 64)
    col = np.zeros((128, PADC), np.float32)
    col[0::2, :COLS] = cos_c.T
    col[1::2, :COLS] = -sin_c.T
    row = np.arange(ALL)
    slot, mode, grid_row, part = row // 24, row // 6 % 2, row // 2 % 3, row % 2
    pick = np.zeros((ALL, 128), np.float32)
    pick[row, slot * 4 + mode * 2 + part] = 1.0
    cos_r, sin_r = tables(ROWS, ROWS)
    device = slot % 16 // 4 * 8 + slot // 16 * 4 + slot % 4
    h = device * 3 + grid_row
    rows_re = np.where(part[None] == 0, cos_r.T[:, h], sin_r.T[:, h])
    rows_im = np.where(part[None] == 0, -sin_r.T[:, h], cos_r.T[:, h])
    rowmix = np.concatenate([rows_re, rows_im])
    return col, pick, rowmix


def floor_div(v, n):
    return jnp.floor((v.astype(F32) + 0.5) * (1.0 / n)).astype(jnp.int32)


def class_mod4(v, n):
    return floor_div(v, n) & 3


def iota(shape, dim):
    return lax.broadcasted_iota(jnp.int32, shape, dim)


def dot(a, b, dims=(((1,), (0,)), ((), ()))):
    return lax.dot_general(a, b, dims, preferred_element_type=F32)


def kernel(
    tok_hbm, cot_hbm, col_ref, colt_ref, pick_ref, pickt_ref, mix_ref, mixt_ref,
    win_ref, wout_ref, bin_ref, bout_ref,
    mixed_ref, tgrad_ref, grads_ref,
    tok, cot, padded, fwd, inv, mrow, mback, wbd,
    send, recv, spec, dgelu, hid, incpair, prepair, work,
    gsrc, gpeer, grs, gplane, gz, gzsum, gpair, gfin, gzag,
    in_sem, send_sem, recv_sem,
):
    me = lax.axis_index("seq")
    rep = lax.axis_index("rep")
    X, Z, Y = me // 8, (me // 4) % 2, me % 4
    xy = X * 4 + Y
    slot = Z * 16 + xy
    zl, core = rep // 2, rep % 2

    def seq_of(z, p):
        return (p // 4) * 8 + z * 4 + p % 4

    def remote(src, dst, k, **where):
        return pltpu.make_async_remote_copy(
            src_ref=src, dst_ref=dst, send_sem=send_sem.at[k], recv_sem=recv_sem.at[k],
            device_id=where, device_id_type=MESH,
        )

    def take(ref, sem):
        pltpu.make_async_copy(ref, ref, sem).wait()

    loads = []
    for s in range(2):
        for h in range(3):
            loads.append(pltpu.make_async_copy(
                tok_hbm.at[s, h], tok.at[s * 3 + h], in_sem.at[0, s * 3 + h]))
    for s in range(2):
        for h in range(3):
            loads.append(pltpu.make_async_copy(
                cot_hbm.at[s, h], cot.at[s * 3 + h], in_sem.at[1, s * 3 + h]))
    for c in loads:
        c.start()
    for sh in range(6):
        padded[sh * PADC + 176:(sh + 1) * PADC, :] = jnp.zeros((16, D), BF)

    barrier = pltpu.get_barrier_semaphore()

    def greet(t, _):
        p = lax.rem(me + t, SLOTS)
        pl.semaphore_signal(barrier, inc=1, device_id={"seq": p}, device_id_type=MESH)
        return 0

    lax.fori_loop(1, SLOTS, greet, 0)
    pl.semaphore_signal(barrier, inc=1, device_id={"rep": zl * 2 + 1 - core}, device_id_type=MESH)
    for t in range(1, 4):
        pl.semaphore_signal(
            barrier, inc=1, device_id={"rep": lax.rem(zl + t, 4) * 2 + core}, device_id_type=MESH)

    picked = dot(pick_ref[...], col_ref[...])
    r = iota((ALL, 1), 0)
    row_sh = class_mod4(r, 12) % 2 * 3 + (floor_div(r, 2) - 3 * floor_div(r, 6))
    for sh in range(6):
        fwd[:, sh * PADC:(sh + 1) * PADC] = jnp.where(row_sh == sh, picked, 0.0).astype(BF)

    pl.semaphore_wait(barrier, SLOTS - 1 + 1 + 3)

    scale_rows = jnp.where((floor_div(r, 24) == 0) & (class_mod4(r, 6) % 2 == 0), 1.0, 2.0)

    def scatter(k):
        def cross(t, _):
            p = lax.rem(xy + t, PLANE)
            remote(send.at[k, (1 - Z) * PLANE + p], recv.at[k, slot], k,
                   seq=seq_of(1 - Z, p)).start()
            return 0

        def near(t, _):
            p = lax.rem(xy + t, PLANE)
            remote(send.at[k, Z * PLANE + p], recv.at[k, slot], k, seq=seq_of(Z, p)).start()
            return 0

        return cross, near

    def store_half(k, z, lhs, rhs, scale):
        left = lhs[pl.ds(pl.multiple_of(z * HALF, HALF), HALF), :]

        def tile(n, _):
            at = pl.ds(pl.multiple_of(n * 256, 256), 256)
            out = dot(left, rhs[:, at])
            if scale is not None:
                out = out * scale
            send[k, pl.ds(z * PLANE, PLANE), :, at] = out.astype(BF).reshape(PLANE, PIECE, 256)
            return 0

        lax.fori_loop(0, 3, tile, 0)

    def exchange(k, lhs, rhs, scale):
        cross, near = scatter(k)
        store_half(k, 1 - Z, lhs, rhs, scale(1 - Z) if scale else None)
        lax.fori_loop(0, PLANE, cross, 0)
        store_half(k, Z, lhs, rhs, scale(Z) if scale else None)
        lax.fori_loop(1, PLANE, near, 0)
        recv[k, slot] = send[k, slot]

    def await_recv(k):
        take(recv.at[k, pl.ds(0, SLOTS - 1)], recv_sem.at[k])

    def await_send(k):
        take(send.at[k, pl.ds(0, SLOTS - 1)], send_sem.at[k])

    def pad(copies, data):
        for sh in range(6):
            copies[sh].wait()
            padded[sh * PADC:sh * PADC + COLS, :] = data[sh]

    pad(loads[:6], tok)
    exchange(0, fwd, padded, None)
    pad(loads[6:], cot)
    rr = iota((HALF, 1), 0)

    def cot_scale(z):
        first = (floor_div(rr, 24) == 0) & (class_mod4(rr, 6) % 2 == 0) & (z == 0)
        return jnp.where(first, 1.0, 2.0)

    exchange(1, fwd, padded, cot_scale)

    c768 = iota((1, ALL), 1)
    col_sh = class_mod4(c768, 12) % 2 * 3 + (floor_div(c768, 2) - 3 * floor_div(c768, 6))
    pickedt = dot(colt_ref[...], pickt_ref[...])
    for sh in range(6):
        inv[sh * PADC:(sh + 1) * PADC, :] = jnp.where(col_sh == sh, pickedt, 0.0).astype(BF)
    col_class = class_mod4(c768, 6)
    row_class = class_mod4(r, 6)
    for e in range(2):
        for cls in range(4):
            at = (e * 4 + cls) * ROWS
            part = mix_ref[e * ROWS:(e + 1) * ROWS, :].astype(F32)
            mrow[at:at + ROWS, :] = jnp.where(col_class == cls, part, 0.0).astype(BF)
    part = mixt_ref[...].astype(F32)
    for e in range(2):
        lane = iota((1, HALF), 1)
        lane_class = floor_div(lane, 96)
        wide = jnp.concatenate([part[:, e * 128:e * 128 + ROWS]] * 4, axis=1)
        mback[:, e * HALF:(e + 1) * HALF] = jnp.where(row_class == lane_class, wide, 0.0).astype(BF)
    lane_block = floor_div(iota((1, HALF), 1), 96)
    for t, ref in enumerate((win_ref, wout_ref)):
        for ri in range(2):
            for g in range(2):
                wide = ref[ri, :, g * HALF:(g + 1) * HALF].astype(F32)
                for n in range(4):
                    wbd[t, ri, g, n * 96:(n + 1) * 96, :] = jnp.where(
                        lane_block == n, wide, 0.0).astype(BF)

    def along_rows(k, store):
        def tile(n, _):
            at = pl.ds(pl.multiple_of(n * 256, 256), 256)
            store(at, dot(mrow[...], recv[k, :, :, at].reshape(ALL, 256)).astype(BF))
            return 0

        lax.fori_loop(0, 3, tile, 0)

    await_recv(0)

    def keep_spec(at, v):
        spec[:, at] = v

    along_rows(0, keep_spec)
    root = math.sqrt(2.0 / math.pi)
    for g in range(2):
        lanes = pl.ds(g * HALF, HALF)
        u = dot(spec[:, lanes], wbd[0, 0, g])
        v = dot(spec[:, lanes], wbd[0, 1, g])
        for e in range(2):
            mine = slice(e * HALF, (e + 1) * HALF)
            if e == 0:
                pre = u[:HALF] - v[HALF:] + bin_ref[0:1, lanes]
            else:
                pre = v[:HALF] + u[HALF:] + bin_ref[1:2, lanes]
            sq = pre * pre
            th = jnp.tanh(root * pre * (1.0 + 0.044715 * sq))
            hid[mine, lanes] = (0.5 * pre * (1.0 + th)).astype(BF)
            dgelu[mine, lanes] = 0.5 * (1.0 + th) + 0.5 * pre * (1.0 - th * th) * (
                root * (1.0 + 3.0 * 0.044715 * sq))
    for g in range(2):
        lanes = pl.ds(g * HALF, HALF)
        u = dot(hid[:, lanes], wbd[1, 0, g])
        v = dot(hid[:, lanes], wbd[1, 1, g])
        work[0:HALF, lanes] = (u[:HALF] - v[HALF:] + bout_ref[0:1, lanes]).astype(BF)
        work[HALF:ALL, lanes] = (v[:HALF] + u[HALF:] + bout_ref[1:2, lanes]).astype(BF)

    def mode_scale(z):
        first = (class_mod4(rr, 6) % 2 == 0) & (slot == 0)
        return jnp.where(first, 1.0, 2.0)

    exchange(2, mback, work, mode_scale)

    await_recv(1)

    def keep_inc(at, v):
        work[:, at] = v

    along_rows(1, keep_inc)

    def pair_up(dst, g, top, bottom):
        dst[g, 0:HALF, 0:HALF] = top
        dst[g, HALF:ALL, 0:HALF] = bottom
        dst[g, 0:HALF, HALF:ALL] = bottom
        dst[g, HALF:ALL, HALF:ALL] = -top

    gsrc[...] = jnp.zeros_like(gsrc)

    def param_grads(t, g, left, pair, bias):
        prod = dot(left[:, g * HALF:(g + 1) * HALF], pair[g], TN)
        for ri in range(2):
            acc = jnp.zeros((96, HALF), F32)
            for n in range(4):
                acc = acc + jnp.where(
                    lane_block == n, prod[n * 96:(n + 1) * 96, ri * HALF:(ri + 1) * HALF], 0.0)
            gsrc[g, t * 8 + ri * 4:t * 8 + ri * 4 + 4, 0:24, :] = acc.reshape(4, 24, HALF)
            gsrc[g, t * 2 + ri, 24:32, :] = jnp.broadcast_to(bias[ri], (8, HALF))

    for g in range(2):
        lanes = pl.ds(g * HALF, HALF)
        inc = work[:, lanes]
        pair_up(incpair, g, inc[:HALF], inc[HALF:])
        u = dot(inc, wbd[1, 0, g], NT)
        v = dot(inc, wbd[1, 1, g], NT)
        top = ((u[:HALF] + v[HALF:]) * dgelu[0:HALF, lanes]).astype(BF)
        bottom = ((u[HALF:] - v[:HALF]) * dgelu[HALF:ALL, lanes]).astype(BF)
        pair_up(prepair, g, top, bottom)
        incf = inc.astype(F32)
        param_grads(1, g, hid, incpair,
                    [jnp.sum(incf[:HALF], axis=0, keepdims=True),
                     jnp.sum(incf[HALF:], axis=0, keepdims=True)])
        param_grads(0, g, spec, prepair,
                    [jnp.sum(top.astype(F32), axis=0, keepdims=True),
                     jnp.sum(bottom.astype(F32), axis=0, keepdims=True)])
    swap = remote(gsrc.at[1 - core], gpeer, 4, rep=zl * 2 + 1 - core)
    swap.start()
    for g in range(2):
        lanes = pl.ds(g * HALF, HALF)
        pre = prepair[g, :, 0:HALF]
        u = dot(pre, wbd[0, 0, g], NT)
        v = dot(pre, wbd[0, 1, g], NT)
        work[0:HALF, lanes] = (u[:HALF] + v[HALF:]).astype(BF)
        work[HALF:ALL, lanes] = (u[HALF:] - v[:HALF]).astype(BF)

    swap.wait_recv()
    grs_own = gsrc.at[core]
    gpeer[...] = gpeer[...] + grs_own[...]

    def reduce_plane(t, _):
        p = lax.rem(xy + t, PLANE)
        remote(gpeer.at[p], grs.at[xy], 5, seq=seq_of(Z, p)).start()
        return 0

    lax.fori_loop(1, PLANE, reduce_plane, 0)
    exchange(3, mback, work, None)

    grs[xy] = gpeer[xy]
    take(grs.at[pl.ds(0, PLANE - 1)], recv_sem.at[5])
    gplane[...] = jnp.sum(grs[...], axis=0).reshape(4, 8, HALF)
    for t in range(1, 4):
        q = lax.rem(zl + t, 4)
        remote(gplane.at[q], gz.at[zl], 6, rep=q * 2 + core).start()
    gz[zl] = gplane[zl]
    take(gz.at[pl.ds(0, 3)], recv_sem.at[6])
    gzsum[...] = jnp.sum(gz[...], axis=0)
    pair = remote(gzsum, gpair, 7, seq=seq_of(1 - Z, xy))
    pair.start()
    pair.wait_recv()
    gfin[...] = (gzsum[...] + gpair[...]) * (1.0 / 16.0)
    for t in range(1, 4):
        q = lax.rem(zl + t, 4)
        remote(gfin, gzag.at[zl], 8, rep=q * 2 + core).start()
    gzag[zl] = gfin[...]
    take(gzag.at[pl.ds(0, 3)], recv_sem.at[8])

    def gather_plane(t, _):
        p = lax.rem(xy + t, PLANE)
        remote(gzag, grads_ref.at[core, xy], 9, seq=seq_of(Z, p)).start()
        return 0

    lax.fori_loop(1, PLANE, gather_plane, 0)
    grads_ref[core, xy] = gzag[...]

    def finish(k, data, out_ref):
        def tile(n, _):
            at = pl.ds(pl.multiple_of(n * 256, 256), 256)
            got = recv[k, :, :, at].reshape(ALL, 256)
            for sh in range(6):
                back = dot(inv[sh * PADC:(sh + 1) * PADC, :], got)
                out_ref[sh // 3, sh % 3, :, at] = (
                    data[sh, :, at].astype(F32) + back[:COLS]).astype(BF)
            return 0

        lax.fori_loop(0, 3, tile, 0)

    await_recv(2)
    finish(2, tok, mixed_ref)

    take(grads_ref.at[core, pl.ds(0, PLANE - 1)], recv_sem.at[9])
    give = remote(grads_ref.at[core], grads_ref.at[core], 10, rep=zl * 2 + 1 - core)
    give.start()

    await_recv(3)
    finish(3, cot, tgrad_ref)
    take(grads_ref.at[1 - core], recv_sem.at[10])

    for k in range(4):
        await_send(k)
    swap.wait_send()
    take(gpeer.at[pl.ds(0, PLANE - 1)], send_sem.at[5])
    take(gplane.at[pl.ds(0, 3)], send_sem.at[6])
    pair.wait_send()
    take(gzag.at[pl.ds(0, 3)], send_sem.at[8])
    take(grads_ref.at[0, pl.ds(0, PLANE - 1)], send_sem.at[9])
    give.wait_send()


def shards(tokens, cotangent, in_weight, in_bias, out_weight, out_bias):
    col, pick, rowmix = constants()
    mixt = np.zeros((ALL, 256), np.float32)
    mixt[:, 0:ROWS] = rowmix[:ROWS].T
    mixt[:, 128:128 + ROWS] = rowmix[ROWS:].T
    const = [jnp.asarray(a, BF) for a in (col, col.T, pick, pick.T, rowmix, mixt)]
    wide = [w.transpose(0, 2, 1, 3).reshape(2, 96, D) for w in (in_weight, out_weight)]
    vm = pl.BlockSpec(memory_space=pltpu.VMEM)
    hb = pl.BlockSpec(memory_space=pl.ANY)
    V = pltpu.VMEM
    grid = tokens.shape
    mixed, tgrad, grads = pl.pallas_call(
        kernel,
        out_shape=(
            jax.ShapeDtypeStruct(grid, BF),
            jax.ShapeDtypeStruct(grid, BF),
            jax.ShapeDtypeStruct((2, PLANE, 4, 8, HALF), F32),
        ),
        in_specs=[hb, hb] + [vm] * 10,
        out_specs=(vm, vm, vm),
        scratch_shapes=[
            V((6, COLS, D), BF), V((6, COLS, D), BF), V((6 * PADC, D), BF),
            V((ALL, 6 * PADC), BF), V((6 * PADC, ALL), BF),
            V((ALL, ALL), BF), V((ALL, ALL), BF),
            V((2, 2, 2, HALF, HALF), BF),
            V((4, SLOTS, PIECE, D), BF), V((4, SLOTS, PIECE, D), BF),
            V((ALL, D), BF), V((ALL, D), F32), V((ALL, D), BF),
            V((2, ALL, ALL), BF), V((2, ALL, ALL), BF), V((ALL, D), BF),
            V((2, PLANE, 32, HALF), F32), V((PLANE, 32, HALF), F32),
            V((PLANE, 32, HALF), F32), V((4, 8, HALF), F32), V((4, 8, HALF), F32),
            V((8, HALF), F32), V((8, HALF), F32), V((8, HALF), F32), V((4, 8, HALF), F32),
            pltpu.SemaphoreType.DMA((2, 6)),
            pltpu.SemaphoreType.DMA((11,)), pltpu.SemaphoreType.DMA((11,)),
        ],
        compiler_params=pltpu.CompilerParams(
            collective_id=0, has_side_effects=True, vmem_limit_bytes=60 * 1024 * 1024),
        name="afno",
    )(tokens, cotangent, *const, *wide, in_bias, out_bias)

    grads = grads.reshape(2, PLANE, 32, HALF)
    full = grads[:, :, 0:24, :].reshape(2, 4, 96, 4, 96).transpose(1, 0, 3, 2, 4)
    full = full.reshape(4, 8, 96, 96)
    bias = grads[:, 0:4, 24, :].transpose(1, 0, 2).reshape(4, D)
    return mixed, tgrad, full[0:2], bias[0:2], full[2:4], bias[2:4]


def solution(mesh):
    in_specs = (P("rep", "seq", None, None), P("rep", "seq", None, None), P(), P(), P(), P())
    out_specs = (P("rep", "seq", None, None), P("rep", "seq", None, None), P(), P(), P(), P())
    return jax.shard_map(shards, mesh=mesh, in_specs=in_specs, out_specs=out_specs, check_vma=False)
```

time: 455 us -> 173 us (0.38); the launches traced: 450 us -> 172 us
  waiting for transfers between devices: 293 us -> 0 us
  Pallas kernels: 0 us -> 154 us
  local copies, waits for them, and re-layouts: 69.5 us -> 17.2 us
  starting transfers between devices: 42.8 us -> 0 us
  matrix products: 21.1 us -> 0 us
  between operations: 15 us -> 0.72 us
  other arithmetic: 7.98 us -> 0 us
    psum x1 -> x0, waiting for transfers between devices: 273 us -> none  [packed_total(): running = lax.psum(ravelled, axis)]
    pallas_call x0 -> x1, Pallas kernels: none -> 154 us  [shards(): pl.pallas_call(kernel, out_shape=(jax.ShapeDtypeStruct(grid, BF), jax.Sha...]
    all_to_all x4 -> x0, starting transfers between devices: 42.7 us -> none  [the longest x1 14.6 us: shards(): lax.all_to_all(spec_rows, 'seq', split_axis=2, concat_axis=1, tiled=True)]
    dot_general x14 -> x0, matrix products: 21.1 us -> none  [the longest x1 4.32 us: mix_forward(): jnp.einsum('mcbi,bciej->mebj', hidden, weights_out, preferred_element_typ...]
    all_to_all x4 -> x0, waiting for transfers between devices: 19.9 us -> none  [the longest x1 19.5 us: shards(): lax.all_to_all(spec_rows, 'seq', split_axis=2, concat_axis=1, tiled=True)]
    convert_element_type x8 -> x0, local copies, waits for them, and re-layouts: 18.2 us -> none  [the longest x2 4.47 us: back_rows(): return jnp.einsum('qehc,sqked->shkcd', row_matrix, section, preferred_ele...]
    reshape x7 -> x4, local copies, waits for them, and re-layouts: 19.8 us -> 3.12 us  [the longest x2 2.07 us: shards(): w.transpose(0, 2, 1, 3).reshape(2, 96, D)]
    all_to_all x6 -> x0, local copies, waits for them, and re-layouts: 15.6 us -> none  [the longest x2 6.42 us: shards(): lax.all_to_all(back_rows(spectrum_out), 'seq', split_axis=1, concat_axis=...]
  transfers between devices with their start and end apart: 5 -> 0, of which waited for: 3 -> 0; matrix products, arithmetic and copies ran while one was open for 10% -> 0% of each run, Pallas kernels for 0% -> 0%
where the time goes in v1:
time: 173 us; the launch traced here: 172 us
  Pallas kernels  154 us (89%)
  local copies, waits for them, and re-layouts  17.2 us (10%)
    pallas_call x1, Pallas kernels, shards(): pl.pallas_call(kernel, out_shape=(jax.ShapeDtypeStruct(grid, BF), jax.Sha...  154 us
    unnamed x15, local copies, waits for them, and re-layouts  10.6 us

profile of v1, /device:TPU:1, one launch (start us, length us, event | category | flops | bytes accessed | tf_op | source)
XLA Modules:
  0.0 172.3 jit_solution(14855172381011003728)
XLA Ops:
  0.6 0.0 copy-start.4
  0.6 0.0 copy-start.1
  0.7 1.3 copy.18
  1.9 1.0 reshape.30.win_ref
  3.0 0.0 copy-done.4
  3.0 0.2 copy.19
  3.1 1.0 reshape.31.wout_ref
  4.2 0.0 copy-done.1
  4.2 0.0 copy-start.2
  4.2 1.4 copy.20.tok_hbm
  5.6 0.6 copy-done.2
  6.2 1.4 copy.21.cot_hbm
  7.6 154.4 %afno.1 = (bf16[2,3,180,768]{3,2,1,0:T(8,128)(2,1)}, bf16[2,3,180,768]{3,2,1,0:T(8,128)(2,1)}, f32[2,16,4,8,384]{4,3,2,1,0:T(8,128)}) custom-call(bf16[2,3,180,768]{3,2,1,0:T(8,128)(2,1)} %copy.20.tok_hbm, bf16[2,3,180,768]{3,2,1,0:T(8,128)(2,1)} %copy.21.cot_hbm, bf16[128,192]{1,0:T(8,128)(2,1)} %constant.12.clone.col_ref, ...), custom_call_target="tpu_custom_call" | custom-call | tf_op jit(solution)/shard_map/afno/pallas_call | solution.py:397
  162.1 0.0 copy-start.3
  162.1 4.0 %copy.25 = bf16[2,3,180,768]{3,0,2,1:T(2,128)(2,1)} copy(bf16[2,3,180,768]{3,2,1,0:T(8,128)(2,1)} %get-tuple-element.12) | data formatting | bytes 3317760
  166.1 0.0 copy-done.3
  166.1 0.1 slice.40
  166.2 0.6 fusion.1
  166.8 0.9 reshape.33
  167.7 0.2 copy.30
  167.9 0.0 copy-start
  167.9 1.3 fusion
  169.2 0.7 copy-done
  169.9 2.4 %copy.26 = bf16[2,3,180,768]{3,0,2,1:T(2,128)(2,1)} copy(bf16[2,3,180,768]{3,2,1,0:T(8,128)(2,1)S(1)} %copy-done) | data formatting | bytes 3317760
  (2 shorter events, 0.0 us)
Async XLA Ops:
  0.6 2.4 %copy-start.4 = (bf16[2,8,96,96]{3,2,1,0:T(8,128)(2,1)S(1)}, bf16[2,8,96,96]{3,2,1,0:T(8,128)(2,1)}, u32[]{:S(2)}) copy-start(bf16[2,8,96,96]{3,2,1,0:T(8,128)(2,1)} %param.16) | copy-start | bytes 884740
  0.6 3.5 %copy-start.1 = (bf16[2,3,180,768]{3,0,2,1:T(2,128)(2,1)S(1)}, bf16[2,3,180,768]{3,0,2,1:T(2,128)(2,1)}, u32[]{:S(2)}) copy-start(bf16[2,3,180,768]{3,0,2,1:T(2,128)(2,1)} %param.12) | copy-start | bytes 4976644
  4.2 2.1 %copy-start.2 = (bf16[2,3,180,768]{3,0,2,1:T(2,128)(2,1)S(1)}, bf16[2,3,180,768]{3,0,2,1:T(2,128)(2,1)}, u32[]{:S(2)}) copy-start(bf16[2,3,180,768]{3,0,2,1:T(2,128)(2,1)} %param.13) | copy-start | bytes 4976644
  162.1 4.0 %copy-start.3 = (f32[2,16,4,8,384]{4,3,2,1,0:T(8,128)S(1)}, f32[2,16,4,8,384]{4,3,2,1,0:T(8,128)}, u32[]{:S(2)}) copy-start(f32[2,16,4,8,384]{4,3,2,1,0:T(8,128)} %get-tuple-element.11) | copy-start | bytes 4718596
  167.9 2.0 %copy-start = (bf16[2,3,180,768]{3,2,1,0:T(8,128)(2,1)S(1)}, bf16[2,3,180,768]{3,2,1,0:T(8,128)(2,1)}, u32[]{:S(2)}) copy-start(bf16[2,3,180,768]{3,2,1,0:T(8,128)(2,1)} %get-tuple-element.13) | copy-start | bytes 4976644

commit v2 on v1

v2 whole, which is shorter than its diff:
```python
import functools
import math

import jax
import jax.numpy as jnp
import numpy as np
from jax import lax
from jax.experimental import pallas as pl
from jax.experimental.pallas import tpu as pltpu
from jax.sharding import PartitionSpec as P

BF = jnp.bfloat16
F32 = jnp.float32
MESH = pl.DeviceIdType.MESH

SLOTS = 32
PLANE = 16
PIECE = 24
ALL = SLOTS * PIECE
D = 768
HALF = 384
COLS = 180
PADR = 384
USED = 360
ROWS = 96
FIRST, SECOND = 6, 11
NT = (((1,), (1,)), ((), ()))
TN = (((0,), (0,)), ((), ()))


def tables(length, modes):
    residue = np.arange(length)[:, None] * np.arange(modes)[None, :] % length
    angles = residue.astype(np.float32) * np.float32(2.0 * math.pi / length)
    factor = np.float32(1.0 / math.sqrt(length))
    return np.cos(angles) * factor, np.sin(angles) * factor


def constants():
    cos_c, sin_c = tables(COLS, 64)
    col = np.zeros((128, PADR), np.float32)
    col[0::2, :USED] = np.repeat(cos_c.T, 2, axis=1)
    col[1::2, :USED] = np.repeat(-sin_c.T, 2, axis=1)
    row = np.arange(ALL)
    slot, grid_row, part = row // 24, row // 2 % 3, row % 2
    cos_r, sin_r = tables(ROWS, ROWS)
    device = slot % 16 // 4 * 8 + slot // 16 * 4 + slot % 4
    h = device * 3 + grid_row
    rows_re = np.where(part[None] == 0, cos_r.T[:, h], sin_r.T[:, h])
    rows_im = np.where(part[None] == 0, -sin_r.T[:, h], cos_r.T[:, h])
    mixt = np.zeros((ALL, 256), np.float32)
    mixt[:, 0:ROWS] = rows_re.T
    mixt[:, 128:128 + ROWS] = rows_im.T
    return col, col.T, np.concatenate([rows_re, rows_im]), mixt


def floor_div(v, n):
    return jnp.floor((v.astype(F32) + 0.5) * (1.0 / n)).astype(jnp.int32)


def class_mod4(v, n):
    return floor_div(v, n) & 3


def iota(shape, dim):
    return lax.broadcasted_iota(jnp.int32, shape, dim)


def dot(a, b, dims=(((1,), (0,)), ((), ()))):
    return lax.dot_general(a, b, dims, preferred_element_type=F32)


def kernel(
    tok_hbm, cot_hbm, col_ref, colt_hbm, mix_hbm, mixt_hbm, win_hbm, wout_hbm, bin_ref, bout_ref,
    mixed_hbm, tgrad_hbm, grads_ref,
    tok, cot, tokp, cotp, colt_ref, mix_ref, mixt_ref, wraw, fwd, inv, mrow, mback, wbd,
    send, recv, spec, dgelu, hid, incpair, prepair, work,
    gsrc, gpeer, grs, gplane, gz, gfin, gzag, gout,
    in_sem, table_sem, out_sem, send_sem, recv_sem,
):
    me = lax.axis_index("seq")
    rep = lax.axis_index("rep")
    X, Z, Y = me // 8, (me // 4) % 2, me % 4
    xy = X * 4 + Y
    slot = Z * 16 + xy
    zl, core = rep // 2, rep % 2

    def seq_of(z, p):
        return (p // 4) * 8 + z * 4 + p % 4

    def remote(src, dst, k, **where):
        return pltpu.make_async_remote_copy(
            src_ref=src, dst_ref=dst, send_sem=send_sem.at[k], recv_sem=recv_sem.at[k],
            device_id=where, device_id_type=MESH,
        )

    def take(ref, sem):
        pltpu.make_async_copy(ref, ref, sem).wait()

    loads = [
        [pltpu.make_async_copy(src.at[h], dst.at[h], in_sem.at[i, h]) for h in range(3)]
        for i, (src, dst) in enumerate(((tok_hbm, tok), (cot_hbm, cot)))
    ]
    late = [
        pltpu.make_async_copy(src, dst, table_sem.at[i])
        for i, (src, dst) in enumerate((
            (colt_hbm, colt_ref), (mix_hbm, mix_ref), (mixt_hbm, mixt_ref),
            (win_hbm, wraw.at[0]), (wout_hbm, wraw.at[1])))
    ]
    for c in loads[0] + loads[1] + late:
        c.start()
    for ref in (tokp, cotp):
        for h in range(3):
            ref[h * PADR + 352:(h + 1) * PADR, :] = jnp.zeros((32, D), BF)

    barrier = pltpu.get_barrier_semaphore()

    def greet(t, _):
        p = lax.rem(me + t, SLOTS)
        pl.semaphore_signal(barrier, inc=1, device_id={"seq": p}, device_id_type=MESH)
        return 0

    lax.fori_loop(1, SLOTS, greet, 0)
    pl.semaphore_signal(barrier, inc=1, device_id={"rep": zl * 2 + 1 - core}, device_id_type=MESH)
    z_here = Z * 4 + zl

    def along_z(t):
        z = lax.rem(z_here + t, 8)
        return z, z // 4, z % 4

    def z_peer(t):
        z, hi, lo = along_z(t)
        return {"seq": seq_of(hi, xy), "rep": lo * 2 + core}

    for t in (1, 2, 3, 5, 6, 7):
        pl.semaphore_signal(barrier, inc=1, device_id=z_peer(t), device_id_type=MESH)

    def message_parts(v):
        cls = class_mod4(v, 6)
        pair = floor_div(v, 2)
        grid_row = pair - 3 * floor_div(v, 6)
        table_row = floor_div(v, 24) * 4 + (cls & 1) * 2 + (v & 1)
        return cls, cls >> 1, grid_row, table_row

    r = iota((ALL, 1), 0)
    row_class, row_s, row_h, row_t = message_parts(r)
    pick = jnp.where(iota((ALL, 128), 1) == row_t, 1.0, 0.0).astype(BF)
    picked = dot(pick, col_ref[...])
    picked = jnp.where((iota((1, PADR), 1) & 1) == row_s, picked, 0.0)
    for h in range(3):
        fwd[:, h * PADR:(h + 1) * PADR] = jnp.where(row_h == h, picked, 0.0).astype(BF)

    def pad(copies, data, ref):
        for h in range(3):
            copies[h].wait()
            ref[h * PADR:h * PADR + USED, :] = data[h].reshape(USED, D)

    pad(loads[0], tok, tokp)
    pl.semaphore_wait(barrier, SLOTS - 1 + 1 + 6)

    def cross(k, lo, hi):
        def step(t, _):
            p = lax.rem(xy + t, PLANE)
            remote(send.at[k, (1 - Z) * PLANE + p], recv.at[k, slot], k,
                   seq=seq_of(1 - Z, p)).start()
            return 0

        lax.fori_loop(lo, hi, step, 0)

    def near(k):
        def step(t, _):
            p = lax.rem(xy + t, PLANE)
            remote(send.at[k, Z * PLANE + p], recv.at[k, slot], k, seq=seq_of(Z, p)).start()
            return 0

        lax.fori_loop(1, PLANE, step, 0)

    def store_half(k, z, lhs, rhs, scale):
        left = lhs[pl.ds(pl.multiple_of(z * HALF, HALF), HALF), :]

        def tile(n, _):
            at = pl.ds(pl.multiple_of(n * 256, 256), 256)
            out = dot(left, rhs[:, at])
            if scale is not None:
                out = out * scale
            send[k, pl.ds(z * PLANE, PLANE), :, at] = out.astype(BF).reshape(PLANE, PIECE, 256)
            return 0

        lax.fori_loop(0, 3, tile, 0)

    def exchange(k, lhs, rhs, scale, first=PLANE):
        store_half(k, 1 - Z, lhs, rhs, scale(1 - Z) if scale else None)
        cross(k, 0, first)
        store_half(k, Z, lhs, rhs, scale(Z) if scale else None)
        near(k)
        recv[k, slot] = send[k, slot]

    def await_recv(k):
        take(recv.at[k, pl.ds(0, SLOTS - 1)], recv_sem.at[k])

    def await_send(k):
        take(send.at[k, pl.ds(0, SLOTS - 1)], send_sem.at[k])

    exchange(0, fwd, tokp, None)
    pad(loads[1], cot, cotp)
    rr = iota((HALF, 1), 0)

    def cot_scale(z):
        first = (floor_div(rr, 24) == 0) & (class_mod4(rr, 6) % 2 == 0) & (z == 0)
        return jnp.where(first, 1.0, 2.0)

    exchange(1, fwd, cotp, cot_scale)

    for c in late:
        c.wait()
    c768 = iota((1, ALL), 1)
    col_class, col_s, col_h, col_t = message_parts(c768)
    pickt = jnp.where(iota((128, ALL), 0) == col_t, 1.0, 0.0).astype(BF)
    pickedt = dot(colt_ref[...], pickt)
    pickedt = jnp.where((iota((PADR, 1), 0) & 1) == col_s, pickedt, 0.0)
    for h in range(3):
        inv[h * PADR:(h + 1) * PADR, :] = jnp.where(col_h == h, pickedt, 0.0).astype(BF)
    for e in range(2):
        part = mix_ref[e * ROWS:(e + 1) * ROWS, :].astype(F32)
        for cls in range(4):
            at = (e * 4 + cls) * ROWS
            mrow[at:at + ROWS, :] = jnp.where(col_class == cls, part, 0.0).astype(BF)
    lane_block = floor_div(iota((1, HALF), 1), 96)
    part = mixt_ref[...].astype(F32)
    for e in range(2):
        wide = jnp.concatenate([part[:, e * 128:e * 128 + ROWS]] * 4, axis=1)
        mback[:, e * HALF:(e + 1) * HALF] = jnp.where(row_class == lane_block, wide, 0.0).astype(BF)
    for n in range(4):
        shift = jnp.where(iota((96, HALF), 1) == iota((96, HALF), 0) + 96 * n, 1.0, 0.0).astype(BF)
        for t in range(2):
            for ri in range(2):
                for g in range(2):
                    wbd[t, ri, g, n * 96:(n + 1) * 96, :] = dot(
                        wraw[t, ri, g * 4 + n], shift).astype(BF)

    def along_rows(k, store):
        def tile(n, _):
            at = pl.ds(pl.multiple_of(n * 256, 256), 256)
            store(at, dot(mrow[...], recv[k, :, :, at].reshape(ALL, 256)).astype(BF))
            return 0

        lax.fori_loop(0, 3, tile, 0)

    await_recv(0)

    def keep_spec(at, v):
        spec[:, at] = v

    along_rows(0, keep_spec)
    root = math.sqrt(2.0 / math.pi)
    for g in range(2):
        lanes = pl.ds(g * HALF, HALF)
        u = dot(spec[:, lanes], wbd[0, 0, g])
        v = dot(spec[:, lanes], wbd[0, 1, g])
        for e in range(2):
            mine = slice(e * HALF, (e + 1) * HALF)
            if e == 0:
                pre = u[:HALF] - v[HALF:] + bin_ref[0:1, lanes]
            else:
                pre = v[:HALF] + u[HALF:] + bin_ref[1:2, lanes]
            sq = pre * pre
            th = jnp.tanh(root * pre * (1.0 + 0.044715 * sq))
            hid[mine, lanes] = (0.5 * pre * (1.0 + th)).astype(BF)
            dgelu[mine, lanes] = 0.5 * (1.0 + th) + 0.5 * pre * (1.0 - th * th) * (
                root * (1.0 + 3.0 * 0.044715 * sq))
    for g in range(2):
        lanes = pl.ds(g * HALF, HALF)
        u = dot(hid[:, lanes], wbd[1, 0, g])
        v = dot(hid[:, lanes], wbd[1, 1, g])
        work[0:HALF, lanes] = (u[:HALF] - v[HALF:] + bout_ref[0:1, lanes]).astype(BF)
        work[HALF:ALL, lanes] = (v[:HALF] + u[HALF:] + bout_ref[1:2, lanes]).astype(BF)

    def mode_scale(z):
        first = (class_mod4(rr, 6) % 2 == 0) & (slot == 0)
        return jnp.where(first, 1.0, 2.0)

    exchange(2, mback, work, mode_scale)

    await_recv(1)

    def keep_inc(at, v):
        work[:, at] = v

    along_rows(1, keep_inc)

    def pair_up(dst, g, top, bottom):
        dst[g, 0:HALF, 0:HALF] = top
        dst[g, HALF:ALL, 0:HALF] = bottom
        dst[g, 0:HALF, HALF:ALL] = bottom
        dst[g, HALF:ALL, HALF:ALL] = -top

    gsrc[...] = jnp.zeros_like(gsrc)

    def param_grads(t, g, left, pair, bias):
        prod = dot(left[:, g * HALF:(g + 1) * HALF], pair[g], TN)
        for ri in range(2):
            acc = jnp.zeros((96, HALF), F32)
            for n in range(4):
                acc = acc + jnp.where(
                    lane_block == n, prod[n * 96:(n + 1) * 96, ri * HALF:(ri + 1) * HALF], 0.0)
            gsrc[g, t * 8 + ri * 4:t * 8 + ri * 4 + 4, 0:24, :] = acc.reshape(4, 24, HALF)
            gsrc[g, t * 2 + ri, 24:32, :] = jnp.broadcast_to(bias[ri], (8, HALF))

    for g in range(2):
        lanes = pl.ds(g * HALF, HALF)
        inc = work[:, lanes]
        pair_up(incpair, g, inc[:HALF], inc[HALF:])
        u = dot(inc, wbd[1, 0, g], NT)
        v = dot(inc, wbd[1, 1, g], NT)
        top = ((u[:HALF] + v[HALF:]) * dgelu[0:HALF, lanes]).astype(BF)
        bottom = ((u[HALF:] - v[:HALF]) * dgelu[HALF:ALL, lanes]).astype(BF)
        pair_up(prepair, g, top, bottom)
        incf = inc.astype(F32)
        param_grads(1, g, hid, incpair,
                    [jnp.sum(incf[:HALF], axis=0, keepdims=True),
                     jnp.sum(incf[HALF:], axis=0, keepdims=True)])
        param_grads(0, g, spec, prepair,
                    [jnp.sum(top.astype(F32), axis=0, keepdims=True),
                     jnp.sum(bottom.astype(F32), axis=0, keepdims=True)])
    swap = remote(gsrc.at[1 - core], gpeer, 4, rep=zl * 2 + 1 - core)
    swap.start()
    for g in range(2):
        lanes = pl.ds(g * HALF, HALF)
        pre = prepair[g, :, 0:HALF]
        u = dot(pre, wbd[0, 0, g], NT)
        v = dot(pre, wbd[0, 1, g], NT)
        work[0:HALF, lanes] = (u[:HALF] + v[HALF:]).astype(BF)
        work[HALF:ALL, lanes] = (u[HALF:] - v[:HALF]).astype(BF)

    swap.wait_recv()
    grs_own = gsrc.at[core]
    gpeer[...] = gpeer[...] + grs_own[...]

    def reduce_plane(t, _):
        p = lax.rem(xy + t, PLANE)
        remote(gpeer.at[p], grs.at[xy], 5, seq=seq_of(Z, p)).start()
        return 0

    lax.fori_loop(1, PLANE, reduce_plane, 0)
    exchange(3, mback, work, None, FIRST)

    grs[xy] = gpeer[xy]
    take(grs.at[pl.ds(0, PLANE - 1)], recv_sem.at[5])
    gplane[...] = jnp.sum(grs[...], axis=0).reshape(4, 8, HALF)

    def piece(hi, lo):
        return gplane.at[lo, :, pl.ds(pl.multiple_of(hi * 128, 128), 256)]

    for t in range(1, 8):
        z, hi, lo = along_z(t)
        remote(piece(hi, lo), gz.at[z_here], 6, **z_peer(t)).start()
    cross(3, FIRST, SECOND)
    gz[z_here] = gplane[zl, :, pl.ds(pl.multiple_of(Z * 128, 128), 256)]
    take(gz.at[pl.ds(0, 7)], recv_sem.at[6])
    gfin[...] = jnp.sum(gz[...], axis=0) * (1.0 / 16.0)
    for t in range(1, 8):
        remote(gfin, gzag.at[z_here], 7, **z_peer(t)).start()
    cross(3, SECOND, PLANE)
    gzag[z_here] = gfin[...]
    take(gzag.at[pl.ds(0, 7)], recv_sem.at[7])
    for t in range(4):
        gout[t, :, 0:256] = gzag[t]
        gout[t, :, 256:HALF] = gzag[4 + t, :, 128:256]

    def gather_plane(t, _):
        p = lax.rem(xy + t, PLANE)
        remote(gout, grads_ref.at[core, xy], 8, seq=seq_of(Z, p)).start()
        return 0

    lax.fori_loop(1, PLANE, gather_plane, 0)
    grads_ref[core, xy] = gout[...]

    def finish(k, data, stage, out_hbm):
        copies = []
        for h in range(3):
            def tile(n, _):
                at = pl.ds(pl.multiple_of(n * 256, 256), 256)
                back = dot(inv[h * PADR:(h + 1) * PADR, :], recv[k, :, :, at].reshape(ALL, 256))
                total = data[h * PADR:h * PADR + USED, at].astype(F32) + back[:USED]
                stage[h, :, :, at] = total.astype(BF).reshape(COLS, 2, 256)
                return 0

            lax.fori_loop(0, 3, tile, 0)
            copies.append(pltpu.make_async_copy(stage.at[h], out_hbm.at[h], out_sem.at[k - 2, h]))
            copies[-1].start()
        return copies

    await_recv(2)
    outs = finish(2, tokp, tok, mixed_hbm)

    take(grads_ref.at[core, pl.ds(0, PLANE - 1)], recv_sem.at[8])
    give = remote(grads_ref.at[core], grads_ref.at[core], 9, rep=zl * 2 + 1 - core)
    give.start()

    await_recv(3)
    outs += finish(3, cotp, cot, tgrad_hbm)
    take(grads_ref.at[1 - core], recv_sem.at[9])

    for k in range(4):
        await_send(k)
    swap.wait_send()
    take(gpeer.at[pl.ds(0, PLANE - 1)], send_sem.at[5])
    take(gz.at[pl.ds(0, 7)], send_sem.at[6])
    take(gzag.at[pl.ds(0, 7)], send_sem.at[7])
    take(grads_ref.at[0, pl.ds(0, PLANE - 1)], send_sem.at[8])
    give.wait_send()
    for c in outs:
        c.wait()


def shards(tokens, cotangent, in_weight, in_bias, out_weight, out_bias):
    const = [jnp.asarray(a, BF) for a in constants()]
    vm = pl.BlockSpec(memory_space=pltpu.VMEM)
    hb = pl.BlockSpec(memory_space=pl.ANY)
    V = pltpu.VMEM
    local = (3, COLS, 2, D)
    mixed, tgrad, grads = pl.pallas_call(
        kernel,
        out_shape=(
            jax.ShapeDtypeStruct(local, BF),
            jax.ShapeDtypeStruct(local, BF),
            jax.ShapeDtypeStruct((2, PLANE, 4, 8, HALF), F32),
        ),
        in_specs=[hb, hb, vm, hb, hb, hb, hb, hb, vm, vm],
        out_specs=(hb, hb, vm),
        scratch_shapes=[
            V(local, BF), V(local, BF), V((3 * PADR, D), BF), V((3 * PADR, D), BF),
            V((PADR, 128), BF), V((2 * ROWS, ALL), BF), V((ALL, 256), BF), V((2, 2, 8, 96, 96), BF),
            V((ALL, 3 * PADR), BF), V((3 * PADR, ALL), BF),
            V((ALL, ALL), BF), V((ALL, ALL), BF),
            V((2, 2, 2, HALF, HALF), BF),
            V((4, SLOTS, PIECE, D), BF), V((4, SLOTS, PIECE, D), BF),
            V((ALL, D), BF), V((ALL, D), F32), V((ALL, D), BF),
            V((2, ALL, ALL), BF), V((2, ALL, ALL), BF), V((ALL, D), BF),
            V((2, PLANE, 32, HALF), F32), V((PLANE, 32, HALF), F32),
            V((PLANE, 32, HALF), F32), V((4, 8, HALF), F32), V((8, 8, 256), F32),
            V((8, 256), F32), V((8, 8, 256), F32), V((4, 8, HALF), F32),
            pltpu.SemaphoreType.DMA((2, 3)), pltpu.SemaphoreType.DMA((5,)),
            pltpu.SemaphoreType.DMA((2, 3)),
            pltpu.SemaphoreType.DMA((10,)), pltpu.SemaphoreType.DMA((10,)),
        ],
        compiler_params=pltpu.CompilerParams(
            collective_id=0, has_side_effects=True, vmem_limit_bytes=60 * 1024 * 1024),
        name="afno",
    )(tokens.transpose(1, 2, 0, 3), cotangent.transpose(1, 2, 0, 3), *const,
      in_weight, out_weight, in_bias, out_bias)
    mixed, tgrad = (a.transpose(2, 0, 1, 3) for a in (mixed, tgrad))

    grads = grads.reshape(2, PLANE, 32, HALF)
    full = grads[:, :, 0:24, :].reshape(2, 4, 96, 4, 96).transpose(1, 0, 3, 2, 4)
    full = full.reshape(4, 8, 96, 96)
    bias = grads[:, 0:4, 24, :].transpose(1, 0, 2).reshape(4, D)
    return mixed, tgrad, full[0:2], bias[0:2], full[2:4], bias[2:4]


def solution(mesh):
    in_specs = (P("rep", "seq", None, None), P("rep", "seq", None, None), P(), P(), P(), P())
    out_specs = (P("rep", "seq", None, None), P("rep", "seq", None, None), P(), P(), P(), P())
    return jax.shard_map(shards, mesh=mesh, in_specs=in_specs, out_specs=out_specs, check_vma=False)
```

time: 173 us -> 158 us (0.913); the launches traced: 172 us -> 155 us
  Pallas kernels: 154 us -> 145 us
  local copies, waits for them, and re-layouts: 17.2 us -> 9.12 us
    pallas_call x1, Pallas kernels: 154 us -> 145 us  [shards(): pl.pallas_call(kernel, out_shape=(jax.ShapeDtypeStruct(local, BF), jax.Sh...]
    unnamed x15 -> x7, local copies, waits for them, and re-layouts: 10.6 us -> 3.91 us
    reshape x2 -> x0, local copies, waits for them, and re-layouts: 2.07 us -> none  [shards(): w.transpose(0, 2, 1, 3).reshape(2, 96, D)]
where the time goes in v2:
time: 158 us; the launch traced here: 155 us
  Pallas kernels  145 us (92%)
  local copies, waits for them, and re-layouts  9.12 us (6%)
    pallas_call x1, Pallas kernels, shards(): pl.pallas_call(kernel, out_shape=(jax.ShapeDtypeStruct(local, BF), jax.Sh...  145 us
    unnamed x7, local copies, waits for them, and re-layouts  3.91 us

profile of v2, /device:TPU:1, one launch (start us, length us, event | category | flops | bytes accessed | tf_op | source)
XLA Modules:
  0.0 155.3 jit_solution(15416676403483768708)
XLA Ops:
  0.6 145.5 %afno.1 = (bf16[3,180,2,768]{3,2,1,0:T(2,128)(2,1)}, bf16[3,180,2,768]{3,2,1,0:T(2,128)(2,1)}, f32[2,16,4,8,384]{4,3,2,1,0:T(8,128)}) custom-call(bf16[3,180,2,768]{3,2,1,0:T(2,128)(2,1)} %bitcast.22, bf16[3,180,2,768]{3,2,1,0:T(2,128)(2,1)} %bitcast.23, bf16[128,384]{1,0:T(8,128)(2,1)} %constant.8.clone.col_ref, bf16[384,128]{1,0:T(8,128)(2,1)} %constant.9.clone.colt_hbm, ...), custom_call_target="tpu_custom_call" | custom-call | tf_op jit(solution)/shard_map/afno/pallas_call | solution.py:421
  146.1 0.9 slice.42
  147.0 1.4 slice.40
  148.4 0.6 fusion.1
  149.0 0.9 reshape.25
  149.9 0.2 copy.22
  150.1 0.0 copy-start.1
  150.1 1.3 fusion
  151.4 0.7 copy-done.1
  152.1 0.0 copy-start
  152.1 1.2 copy.26
  153.3 0.9 copy-done
  154.1 1.2 copy.27
  (1 shorter events, 0.0 us)
Async XLA Ops:
  150.1 2.0 %copy-start.1 = (bf16[3,180,2,768]{3,2,1,0:T(2,128)(2,1)S(1)}, bf16[3,180,2,768]{3,2,1,0:T(2,128)(2,1)}, u32[]{:S(2)}) copy-start(bf16[3,180,2,768]{3,2,1,0:T(2,128)(2,1)} %get-tuple-element.9) | copy-start | bytes 4976644
  152.1 2.0 %copy-start = (bf16[3,180,2,768]{3,2,1,0:T(2,128)(2,1)S(1)}, bf16[3,180,2,768]{3,2,1,0:T(2,128)(2,1)}, u32[]{:S(2)}) copy-start(bf16[3,180,2,768]{3,2,1,0:T(2,128)(2,1)} %get-tuple-element.10) | copy-start | bytes 4976644

commit v3 on v2

--- a/solution.py
+++ b/solution.py
@@ -23,7 +23,7 @@
 PADR = 384
 USED = 360
 ROWS = 96
-FIRST, SECOND = 6, 11
+WINDOW = 6
 NT = (((1,), (1,)), ((), ()))
 TN = (((0,), (0,)), ((), ()))
 
@@ -71,11 +71,11 @@
 
 def kernel(
     tok_hbm, cot_hbm, col_ref, colt_hbm, mix_hbm, mixt_hbm, win_hbm, wout_hbm, bin_ref, bout_ref,
-    mixed_hbm, tgrad_hbm, grads_ref,
-    tok, cot, tokp, cotp, colt_ref, mix_ref, mixt_ref, wraw, fwd, inv, mrow, mback, wbd,
+    mixed_ref, tgrad_ref, gwin_ref, gbin_ref, gwout_ref, gbout_ref,
+    tok, cot, tokp, cotp, grads_ref, colt_ref, mix_ref, mixt_ref, wraw, fwd, inv, mrow, mback, wbd,
     send, recv, spec, dgelu, hid, incpair, prepair, work,
     gsrc, gpeer, grs, gplane, gz, gfin, gzag, gout,
-    in_sem, table_sem, out_sem, send_sem, recv_sem,
+    in_sem, table_sem, cross_sem, send_sem, recv_sem,
 ):
     me = lax.axis_index("seq")
     rep = lax.axis_index("rep")
@@ -157,11 +157,19 @@
     pad(loads[0], tok, tokp)
     pl.semaphore_wait(barrier, SLOTS - 1 + 1 + 6)
 
-    def cross(k, lo, hi):
+    def await_cross(k, t):
+        pltpu.make_async_copy(send.at[k, 0], send.at[k, 0], cross_sem.at[k, t]).wait()
+
+    def cross(k, lo, hi, paced=False):
         def step(t, _):
+            if paced:
+                before = k * PLANE + t - WINDOW
+                await_cross(before // PLANE, before % PLANE)
             p = lax.rem(xy + t, PLANE)
-            remote(send.at[k, (1 - Z) * PLANE + p], recv.at[k, slot], k,
-                   seq=seq_of(1 - Z, p)).start()
+            pltpu.make_async_remote_copy(
+                src_ref=send.at[k, (1 - Z) * PLANE + p], dst_ref=recv.at[k, slot],
+                send_sem=cross_sem.at[k, t], recv_sem=recv_sem.at[k],
+                device_id={"seq": seq_of(1 - Z, p)}, device_id_type=MESH).start()
             return 0
 
         lax.fori_loop(lo, hi, step, 0)
@@ -187,18 +195,19 @@
 
         lax.fori_loop(0, 3, tile, 0)
 
-    def exchange(k, lhs, rhs, scale, first=PLANE):
+    def exchange(k, lhs, rhs, scale, first=PLANE, paced=False, both=True):
         store_half(k, 1 - Z, lhs, rhs, scale(1 - Z) if scale else None)
-        cross(k, 0, first)
+        cross(k, 0, first, paced)
         store_half(k, Z, lhs, rhs, scale(Z) if scale else None)
-        near(k)
+        if both:
+            near(k)
         recv[k, slot] = send[k, slot]
 
     def await_recv(k):
         take(recv.at[k, pl.ds(0, SLOTS - 1)], recv_sem.at[k])
 
     def await_send(k):
-        take(send.at[k, pl.ds(0, SLOTS - 1)], send_sem.at[k])
+        take(send.at[k, pl.ds(0, PLANE - 1)], send_sem.at[k])
 
     exchange(0, fwd, tokp, None)
     pad(loads[1], cot, cotp)
@@ -208,7 +217,8 @@
         first = (floor_div(rr, 24) == 0) & (class_mod4(rr, 6) % 2 == 0) & (z == 0)
         return jnp.where(first, 1.0, 2.0)
 
-    exchange(1, fwd, cotp, cot_scale)
+    held = jnp.where(z_here % 4 == 0, 11, jnp.where(z_here % 4 == 3, 14, PLANE))
+    exchange(1, fwd, cotp, cot_scale, held)
 
     for c in late:
         c.wait()
@@ -278,14 +288,18 @@
         first = (class_mod4(rr, 6) % 2 == 0) & (slot == 0)
         return jnp.where(first, 1.0, 2.0)
 
-    exchange(2, mback, work, mode_scale)
+    exchange(2, mback, work, mode_scale, 0)
+
+    cross(1, held, PLANE)
 
     await_recv(1)
 
     def keep_inc(at, v):
         work[:, at] = v
 
+    cross(2, 0, WINDOW)
     along_rows(1, keep_inc)
+    cross(2, WINDOW, 8, True)
 
     def pair_up(dst, g, top, bottom):
         dst[g, 0:HALF, 0:HALF] = top
@@ -314,6 +328,7 @@
         top = ((u[:HALF] + v[HALF:]) * dgelu[0:HALF, lanes]).astype(BF)
         bottom = ((u[HALF:] - v[:HALF]) * dgelu[HALF:ALL, lanes]).astype(BF)
         pair_up(prepair, g, top, bottom)
+        cross(2, 8 + 3 * g, 11 + 3 * g, True)
         incf = inc.astype(F32)
         param_grads(1, g, hid, incpair,
                     [jnp.sum(incf[:HALF], axis=0, keepdims=True),
@@ -323,6 +338,7 @@
                      jnp.sum(bottom.astype(F32), axis=0, keepdims=True)])
     swap = remote(gsrc.at[1 - core], gpeer, 4, rep=zl * 2 + 1 - core)
     swap.start()
+    cross(2, 14, PLANE, True)
     for g in range(2):
         lanes = pl.ds(g * HALF, HALF)
         pre = prepair[g, :, 0:HALF]
@@ -341,7 +357,7 @@
         return 0
 
     lax.fori_loop(1, PLANE, reduce_plane, 0)
-    exchange(3, mback, work, None, FIRST)
+    exchange(3, mback, work, None, WINDOW, True, False)
 
     grs[xy] = gpeer[xy]
     take(grs.at[pl.ds(0, PLANE - 1)], recv_sem.at[5])
@@ -353,18 +369,19 @@
     for t in range(1, 8):
         z, hi, lo = along_z(t)
         remote(piece(hi, lo), gz.at[z_here], 6, **z_peer(t)).start()
-    cross(3, FIRST, SECOND)
+    near(3)
+    cross(3, WINDOW, 10, True)
     gz[z_here] = gplane[zl, :, pl.ds(pl.multiple_of(Z * 128, 128), 256)]
     take(gz.at[pl.ds(0, 7)], recv_sem.at[6])
     gfin[...] = jnp.sum(gz[...], axis=0) * (1.0 / 16.0)
     for t in range(1, 8):
         remote(gfin, gzag.at[z_here], 7, **z_peer(t)).start()
-    cross(3, SECOND, PLANE)
+    cross(3, 10, PLANE, True)
     gzag[z_here] = gfin[...]
     take(gzag.at[pl.ds(0, 7)], recv_sem.at[7])
     for t in range(4):
-        gout[t, :, 0:256] = gzag[t]
-        gout[t, :, 256:HALF] = gzag[4 + t, :, 128:256]
+        gout[t, :, 0:256] = gzag[t].astype(BF)
+        gout[t, :, 256:HALF] = gzag[4 + t, :, 128:256].astype(BF)
 
     def gather_plane(t, _):
         p = lax.rem(xy + t, PLANE)
@@ -374,41 +391,62 @@
     lax.fori_loop(1, PLANE, gather_plane, 0)
     grads_ref[core, xy] = gout[...]
 
-    def finish(k, data, stage, out_hbm):
-        copies = []
-        for h in range(3):
-            def tile(n, _):
-                at = pl.ds(pl.multiple_of(n * 256, 256), 256)
-                back = dot(inv[h * PADR:(h + 1) * PADR, :], recv[k, :, :, at].reshape(ALL, 256))
+    def finish(k, data, out_ref):
+        def tile(n, _):
+            at = pl.ds(pl.multiple_of(n * 256, 256), 256)
+            got = recv[k, :, :, at].reshape(ALL, 256)
+            for h in range(3):
+                back = dot(inv[h * PADR:(h + 1) * PADR, :], got)
                 total = data[h * PADR:h * PADR + USED, at].astype(F32) + back[:USED]
-                stage[h, :, :, at] = total.astype(BF).reshape(COLS, 2, 256)
-                return 0
-
-            lax.fori_loop(0, 3, tile, 0)
-            copies.append(pltpu.make_async_copy(stage.at[h], out_hbm.at[h], out_sem.at[k - 2, h]))
-            copies[-1].start()
-        return copies
+                out_ref[h, :, :, at] = total.astype(BF).reshape(COLS, 2, 256)
+            return 0
+
+        lax.fori_loop(0, 3, tile, 0)
+
+    def place_grads(g):
+        for q in range(4):
+            weight, bias = ((gwin_ref, gbin_ref), (gwout_ref, gbout_ref))[q // 2]
+            wide = grads_ref[g, 4 * q:4 * q + 4, 0:3].astype(F32).reshape(96, HALF)
+            for n in range(4):
+                weight[q % 2, g * 4 + n] = wide[:, n * 96:(n + 1) * 96]
+            bias[q % 2:q % 2 + 1, pl.ds(pl.multiple_of(g * HALF, 128), HALF)] = (
+                grads_ref[g, q, 3].astype(F32)[0:1])
 
     await_recv(2)
-    outs = finish(2, tokp, tok, mixed_hbm)
+    finish(2, tokp, mixed_ref)
 
     take(grads_ref.at[core, pl.ds(0, PLANE - 1)], recv_sem.at[8])
     give = remote(grads_ref.at[core], grads_ref.at[core], 9, rep=zl * 2 + 1 - core)
     give.start()
-
+    place_grads(core)
     await_recv(3)
-    outs += finish(3, cotp, cot, tgrad_hbm)
+    finish(3, cotp, tgrad_ref)
     take(grads_ref.at[1 - core], recv_sem.at[9])
+    place_grads(1 - core)
 
     for k in range(4):
         await_send(k)
+
+    def drain(u, _):
+        await_cross(u // PLANE, u % PLANE)
+        return 0
+
+    lax.fori_loop(0, 2 * PLANE, drain, 0)
+    lax.fori_loop(4 * PLANE - WINDOW, 4 * PLANE, drain, 0)
     swap.wait_send()
     take(gpeer.at[pl.ds(0, PLANE - 1)], send_sem.at[5])
     take(gz.at[pl.ds(0, 7)], send_sem.at[6])
     take(gzag.at[pl.ds(0, 7)], send_sem.at[7])
     take(grads_ref.at[0, pl.ds(0, PLANE - 1)], send_sem.at[8])
     give.wait_send()
-    for c in outs:
+
+
+def copy_out(*refs):
+    n = len(refs) // 2
+    copies = [pltpu.make_async_copy(refs[i], refs[n + i], refs[-1].at[i]) for i in range(n)]
+    for c in copies:
+        c.start()
+    for c in copies:
         c.wait()
 
 
@@ -418,17 +456,18 @@
     hb = pl.BlockSpec(memory_space=pl.ANY)
     V = pltpu.VMEM
     local = (3, COLS, 2, D)
-    mixed, tgrad, grads = pl.pallas_call(
+    results = pl.pallas_call(
         kernel,
         out_shape=(
-            jax.ShapeDtypeStruct(local, BF),
-            jax.ShapeDtypeStruct(local, BF),
-            jax.ShapeDtypeStruct((2, PLANE, 4, 8, HALF), F32),
+            V(local, BF), V(local, BF),
+            V(in_weight.shape, F32), V(in_bias.shape, F32),
+            V(out_weight.shape, F32), V(out_bias.shape, F32),
         ),
         in_specs=[hb, hb, vm, hb, hb, hb, hb, hb, vm, vm],
-        out_specs=(hb, hb, vm),
+        out_specs=(vm,) * 6,
         scratch_shapes=[
             V(local, BF), V(local, BF), V((3 * PADR, D), BF), V((3 * PADR, D), BF),
+            V((2, PLANE, 4, 8, HALF), BF),
             V((PADR, 128), BF), V((2 * ROWS, ALL), BF), V((ALL, 256), BF), V((2, 2, 8, 96, 96), BF),
             V((ALL, 3 * PADR), BF), V((3 * PADR, ALL), BF),
             V((ALL, ALL), BF), V((ALL, ALL), BF),
@@ -438,23 +477,27 @@
             V((2, ALL, ALL), BF), V((2, ALL, ALL), BF), V((ALL, D), BF),
             V((2, PLANE, 32, HALF), F32), V((PLANE, 32, HALF), F32),
             V((PLANE, 32, HALF), F32), V((4, 8, HALF), F32), V((8, 8, 256), F32),
-            V((8, 256), F32), V((8, 8, 256), F32), V((4, 8, HALF), F32),
+            V((8, 256), F32), V((8, 8, 256), F32), V((4, 8, HALF), BF),
             pltpu.SemaphoreType.DMA((2, 3)), pltpu.SemaphoreType.DMA((5,)),
-            pltpu.SemaphoreType.DMA((2, 3)),
+            pltpu.SemaphoreType.DMA((4, PLANE)),
             pltpu.SemaphoreType.DMA((10,)), pltpu.SemaphoreType.DMA((10,)),
         ],
         compiler_params=pltpu.CompilerParams(
-            collective_id=0, has_side_effects=True, vmem_limit_bytes=60 * 1024 * 1024),
+            collective_id=0, has_side_effects=True, vmem_limit_bytes=54 * 1024 * 1024),
         name="afno",
     )(tokens.transpose(1, 2, 0, 3), cotangent.transpose(1, 2, 0, 3), *const,
       in_weight, out_weight, in_bias, out_bias)
+    mixed, tgrad, *grads = pl.pallas_call(
+        copy_out,
+        out_shape=[jax.ShapeDtypeStruct(a.shape, a.dtype) for a in results],
+        in_specs=[vm] * 6,
+        out_specs=[hb] * 6,
+        scratch_shapes=[pltpu.SemaphoreType.DMA((6,))],
+        compiler_params=pltpu.CompilerParams(vmem_limit_bytes=1024 * 1024),
+        name="copy_out",
+    )(*[pltpu.with_memory_space_constraint(a, pltpu.VMEM) for a in results])
     mixed, tgrad = (a.transpose(2, 0, 1, 3) for a in (mixed, tgrad))
-
-    grads = grads.reshape(2, PLANE, 32, HALF)
-    full = grads[:, :, 0:24, :].reshape(2, 4, 96, 4, 96).transpose(1, 0, 3, 2, 4)
-    full = full.reshape(4, 8, 96, 96)
-    bias = grads[:, 0:4, 24, :].transpose(1, 0, 2).reshape(4, D)
-    return mixed, tgrad, full[0:2], bias[0:2], full[2:4], bias[2:4]
+    return mixed, tgrad, *grads
 
 
 def solution(mesh):

time: 158 us -> 143 us (0.905); the launches traced: 155 us -> 143 us
  local copies, waits for them, and re-layouts: 9.12 us -> 0 us
  Pallas kernels: 145 us -> 142 us
    slice x4 -> x0, local copies, waits for them, and re-layouts: 4.16 us -> none  [the longest x2 1.91 us: shards(): return (mixed, tgrad, full[0:2], bias[0:2], full[2:4], bias[2:4])]
    unnamed x7 -> x0, local copies, waits for them, and re-layouts: 3.91 us -> none
    pallas_call x1 -> x2, Pallas kernels: 145 us -> 142 us  [the longest x1 140 us: shards(): pl.pallas_call(kernel, out_shape=(V(local, BF), V(local, BF), V(in_weight...]
where the time goes in v3:
time: 143 us
  Pallas kernels  142 us (99%)
    pallas_call x1, Pallas kernels, shards(): pl.pallas_call(kernel, out_shape=(V(local, BF), V(local, BF), V(in_weight...  140 us

profile of v3, /device:TPU:1, one launch (start us, length us, event | category | flops | bytes accessed | tf_op | source)
XLA Modules:
  0.0 143.1 jit_solution(16408491813484278329)
XLA Ops:
  0.6 140.0 %afno.1 = (bf16[3,180,2,768]{3,2,1,0:T(2,128)(2,1)S(1)}, bf16[3,180,2,768]{3,2,1,0:T(2,128)(2,1)S(1)}, f32[2,8,96,96]{3,2,1,0:T(8,128)S(1)}, f32[2,768]{1,0:T(2,...) custom-call(bf16[3,180,2,768]{3,2,1,0:T(2,128)(2,1)} %bitcast.4, bf16[3,180,2,768]{3,2,1,0:T(2,128)(2,1)} %bitcast.5, ...), custom_call_target="tpu_custom_call" | custom-call | tf_op jit(solution)/shard_map/afno/pallas_call | solution.py:459
  140.6 2.3 %copy_out.1 = (bf16[3,180,2,768]{3,2,1,0:T(2,128)(2,1)}, bf16[3,180,2,768]{3,2,1,0:T(2,128)(2,1)}, f32[2,8,96,96]{3,2,1,0:T(8,128)}, f32[2,768]{1,0:T(2,128)}, f...) custom-call(bf16[3,180,2,768]{3,2,1,0:T(2,128)(2,1)S(1)} %get-tuple-element.18.refs_0_, ...), custom_call_target="tpu_custom_call" | custom-call | tf_op jit(solution)/shard_map/copy_out/pallas_call | solution.py:490

commit v4 on v3

--- a/solution.py
+++ b/solution.py
@@ -370,13 +370,13 @@
         z, hi, lo = along_z(t)
         remote(piece(hi, lo), gz.at[z_here], 6, **z_peer(t)).start()
     near(3)
-    cross(3, WINDOW, 10, True)
+    cross(3, WINDOW, 13, True)
     gz[z_here] = gplane[zl, :, pl.ds(pl.multiple_of(Z * 128, 128), 256)]
     take(gz.at[pl.ds(0, 7)], recv_sem.at[6])
     gfin[...] = jnp.sum(gz[...], axis=0) * (1.0 / 16.0)
     for t in range(1, 8):
         remote(gfin, gzag.at[z_here], 7, **z_peer(t)).start()
-    cross(3, 10, PLANE, True)
+    cross(3, 13, PLANE, True)
     gzag[z_here] = gfin[...]
     take(gzag.at[pl.ds(0, 7)], recv_sem.at[7])
     for t in range(4):

time: 143 us -> 143 us (level)
  no operation moved by 1% of the time
where the time goes in v4:
time: 143 us
  Pallas kernels  142 us (99%)
    pallas_call x1, Pallas kernels, shards(): pl.pallas_call(kernel, out_shape=(V(local, BF), V(local, BF), V(in_weight...  139 us

profile of v4, /device:TPU:1, one launch (start us, length us, event | category | flops | bytes accessed | tf_op | source)
XLA Modules:
  0.0 142.6 jit_solution(4769351676681130390)
XLA Ops:
  0.6 139.5 %afno.1 = (bf16[3,180,2,768]{3,2,1,0:T(2,128)(2,1)S(1)}, bf16[3,180,2,768]{3,2,1,0:T(2,128)(2,1)S(1)}, f32[2,8,96,96]{3,2,1,0:T(8,128)S(1)}, f32[2,768]{1,0:T(2,...) custom-call(bf16[3,180,2,768]{3,2,1,0:T(2,128)(2,1)} %bitcast.4, bf16[3,180,2,768]{3,2,1,0:T(2,128)(2,1)} %bitcast.5, ...), custom_call_target="tpu_custom_call" | custom-call | tf_op jit(solution)/shard_map/afno/pallas_call | solution.py:459
  140.1 2.3 %copy_out.1 = (bf16[3,180,2,768]{3,2,1,0:T(2,128)(2,1)}, bf16[3,180,2,768]{3,2,1,0:T(2,128)(2,1)}, f32[2,8,96,96]{3,2,1,0:T(8,128)}, f32[2,768]{1,0:T(2,128)}, f...) custom-call(bf16[3,180,2,768]{3,2,1,0:T(2,128)(2,1)S(1)} %get-tuple-element.18.refs_0_, ...), custom_call_target="tpu_custom_call" | custom-call | tf_op jit(solution)/shard_map/copy_out/pallas_call | solution.py:490
